TPU v7x, 32 devices: a whole 2x2x4 slice. The times are simulated.
32 devices in a mesh: tgt: 8 (over y, x, core), src: 4 (over z).
Axes of the slice: x: 2, y: 2, z: 4, core: 2. Of those that a mesh axis runs over, the one named last changes fastest.
Arguments:
- fibre_points: float32 [3, 64, 64], P(None, ('tgt', 'src')), may hold values from -6 to 6
- shell_points: float32 [3, 128, 64], P(None, 'tgt', 'src'), may hold values from -7 to 7, as said below
- bending: float32 [64, 64], replicated, may hold values from -0.12 to 0.12
- shell_inverse: bfloat16 [3, 128, 64, 3, 64, 128], P(None, 'tgt', None, None, 'src'), may hold values from -0.0390625 to 0.0390625
Outputs:
- fibre_velocity: float32 [3, 64, 64], P(None, ('tgt', 'src'))
- shell_density: float32 [3, 128, 64], P(None, 'tgt', 'src')
Inputs may be any that keep to these rules, and one draw needn't show every extreme that they name: `shell_points`: every shell node lies on the sphere of radius 7 about the anchor.
All inputs are finite; a program needn't handle non-finite values.
Results may differ from a plain program's by a relative error of at most 0.0029.
Values may be sent and summed in bfloat16 or wider, within the bound.
A program may use at most 64 MiB of HBM per device.

v0:
```python
import math
import jax
import jax.numpy as jnp
from jax import lax
from jax.sharding import PartitionSpec as P

mobility = 1.0 / (8.0 * math.pi)
soften_sq = 0.0025


def stokes_flow(targets, sources, strength):
    delta_x = targets[0][:, None] - sources[0][None, :]
    delta_y = targets[1][:, None] - sources[1][None, :]
    delta_z = targets[2][:, None] - sources[2][None, :]
    dist_sq = delta_x * delta_x + delta_y * delta_y + delta_z * delta_z
    inv_root = lax.rsqrt(dist_sq + soften_sq)
    inv_cubed = inv_root * inv_root * inv_root
    projection = (
        delta_x * strength[0][None, :]
        + delta_y * strength[1][None, :]
        + delta_z * strength[2][None, :]
    ) * inv_cubed
    diagonal_part = (dist_sq + 2.0 * soften_sq) * inv_cubed
    flow_x = jnp.sum(diagonal_part * strength[0][None, :] + projection * delta_x, axis=1)
    flow_y = jnp.sum(diagonal_part * strength[1][None, :] + projection * delta_y, axis=1)
    flow_z = jnp.sum(diagonal_part * strength[2][None, :] + projection * delta_z, axis=1)
    return mobility * jnp.stack([flow_x, flow_y, flow_z])


def block_width(column_count, target_count):
    widest = 128
    while widest * 2 * target_count <= 1 << 20:
        widest = widest * 2
    return math.gcd(column_count, widest)


def source_sum(running, targets, places, pushes):
    block_size = block_width(places.shape[1], targets.shape[1])
    turns = places.shape[1] // block_size

    def add_block(counter, partial_value):
        offset = counter * block_size
        part_places = lax.dynamic_slice_in_dim(places, offset, block_size, 1)
        part_pushes = lax.dynamic_slice_in_dim(pushes, offset, block_size, 1)
        return partial_value + stokes_flow(targets, part_places, part_pushes)

    return lax.fori_loop(0, turns, add_block, running)


def fibre_fold(targets, running, pieces):
    return source_sum(running, targets, pieces[0].reshape(3, -1), pieces[1].reshape(3, -1))


def per_device(fibre_points, shell_points, bending, shell_inverse):
    shell_rows = lax.all_gather(shell_points, "src", axis=2, tiled=True)
    columns_pos = lax.all_gather(shell_points, "tgt", axis=1, tiled=True)
    forces = -jnp.einsum("cfm,nm->cfn", fibre_points, bending, precision=lax.Precision.HIGHEST)
    fibre_block = lax.all_gather(fibre_points, "src", axis=1, tiled=True)
    block_flat = fibre_block.reshape(3, -1)
    targets = jnp.concatenate([block_flat, shell_rows.reshape(3, -1)], axis=1)
    zeros_flow = jnp.zeros(targets.shape, jnp.float32)
    flow_all = fibre_fold(
        targets,
        zeros_flow,
        (
            lax.all_gather(fibre_points, "tgt", axis=1, tiled=True),
            lax.all_gather(forces, "tgt", axis=1, tiled=True),
        ),
    )
    block_count = block_flat.shape[1]
    fibre_part = flow_all[:, :block_count].reshape(fibre_block.shape)
    shell_part = flow_all[:, block_count:].reshape(shell_rows.shape)
    fibre_flow = lax.psum_scatter(fibre_part, "src", scatter_dimension=1, tiled=True)
    shell_flow = lax.psum_scatter(shell_part, "src", scatter_dimension=2, tiled=True)
    columns = lax.all_gather(shell_flow.astype(jnp.bfloat16), "tgt", axis=1, tiled=True)
    density_rows = -jnp.einsum(
        "xaqcbn,cnb->xaq", shell_inverse, columns, preferred_element_type=jnp.float32
    )
    density = lax.psum_scatter(density_rows, "src", scatter_dimension=2, tiled=True)
    column_density = lax.all_gather(density, "tgt", axis=1, tiled=True)
    zeros_back = jnp.zeros(block_flat.shape, jnp.float32)
    back_block = source_sum(
        zeros_back, block_flat, columns_pos.reshape(3, -1), column_density.reshape(3, -1)
    )
    shell_back = lax.psum_scatter(
        back_block.reshape(fibre_block.shape), "src", scatter_dimension=1, tiled=True
    )
    velocity = fibre_flow + shell_back
    return (velocity, density)


def solution(mesh):
    placed = (
        P(None, ("tgt", "src"), None),
        P(None, "tgt", "src"),
        P(),
        P(None, "tgt", None, None, "src", None),
    )
    return jax.shard_map(
        per_device,
        mesh=mesh,
        in_specs=placed,
        out_specs=(P(None, ("tgt", "src"), None), P(None, "tgt", "src")),
        check_vma=False,
    )
```

profile of v0, /device:TPU:0, one launch (start us, length us, event | category | flops | bytes accessed | tf_op | source)
XLA Modules:
  0.0 174.0 jit_solution(9149982009309895691)
XLA Ops:
  7.2 0.0 copy-start
  7.2 0.0 reduce-scatter.8.cloned.1.call-start
  7.2 0.7 copy.22
  7.9 14.9 %all_gather.21 = f32[3,8,64]{2,0,1:T(4,128)S(1)} all-gather(f32[3,2,64]{2,0,1:T(4,128)S(1)} %copy.22), channel_id=1, replica_groups=mesh['tgt'=8,'src'=4] {'src'}, dimensions={1}, use_global_device_ids=true | all-gather | bytes 7680 | tf_op jit(solution)/shard_map/all_gather | solution.py:58
  22.8 9.1 %all_gather.23 = f32[3,16,64]{2,0,1:T(4,128)S(1)} all-gather(f32[3,2,64]{2,0,1:T(4,128)S(1)} %copy.22), channel_id=1, replica_groups=mesh['tgt'=8,'src'=4] {'tgt'}, dimensions={1}, use_global_device_ids=true | all-gather | bytes 13824 | tf_op jit(solution)/shard_map/all_gather | solution.py:66
  31.9 0.0 copy-done
  31.9 0.8 convolution_negate_fusion
  32.8 0.1 reshape.55
  32.9 0.1 reshape.57
  33.0 9.1 %all_gather.24 = f32[3,16,64]{2,0,1:T(4,128)S(1)} all-gather(f32[3,2,64]{2,0,1:T(4,128)S(1)} %convolution_negate_fusion), channel_id=1, replica_groups=mesh['tgt'=8,'src'=4] {'tgt'}, dimensions={1}, use_global_device_ids=true | all-gather | bytes 13824 | tf_op jit(solution)/shard_map/all_gather | solution.py:67
  42.0 0.1 reshape.58
  42.1 0.8 copy.24
  42.9 13.3 %all_gather.22 = f32[3,16,64]{1,0,2:T(4,128)S(1)} all-gather(f32[3,16,16]{1,0,2:T(4,128)S(1)} %copy.24), channel_id=1, replica_groups=mesh['tgt'=8,'src'=4] {'src'}, dimensions={2}, use_global_device_ids=true | all-gather | bytes 15360 | tf_op jit(solution)/shard_map/all_gather | solution.py:55
  56.3 0.1 copy.25
  56.4 0.1 reshape.56
  56.5 0.0 copy-start.1
  56.5 10.0 %while.9 = (s32[]{:T(128)}, f32[3,1536]{1,0:T(4,128)S(1)}, f32[3,1536]{1,0:T(4,128)S(1)}, f32[3,1024]{1,0:T(4,128)S(1)}, f32[3,1024]{1,0:T(4,128)S(1)}, /*index=...) while((s32[]{:T(128)}, f32[3,1536]{1,0:T(4,128)S(1)}, ...), condition=%wide.region_4.0_spmd.clone, body=%wide.region_0.0_spmd.clone.sunk | while | flops 24397832 | bytes 202961 | solution.py:47
  56.5 0.1 fusion.44
  56.6 0.1 slice_reduce_fusion.7
  56.7 4.7 %fusion.45 = (f32[1536]{0:T(1024)S(1)}, f32[1536]{0:T(1024)S(1)}, f32[1536]{0:T(1024)S(1)}) fusion(f32[512]{0:T(512)S(1)} %bitcast.39, f32[512]{0:T(512)S(1)} %bitcast.42, f32[1536]{0:T(1024)S(1)} %get-tuple-element.215, f32[512]{0:T(512)S(1)} %bitcast.41, f32[1536]{0:T(1024)S(1)} %get-tuple-element.217, f32[512]{0:T(512)S(1)} %bitcast.43, ...), kind=kLoop, calls=%fused_computation.16.clone.1 | loop fusion | flops 24374784 | bytes 49152 | tf_op jit(solution)/shard_map/while/body/eval_jaxpr/reduce_sum | solution.py:24
  61.5 0.1 fusion.44
  61.6 0.1 slice_reduce_fusion.7
  61.7 4.7 %fusion.45 = (f32[1536]{0:T(1024)S(1)}, f32[1536]{0:T(1024)S(1)}, f32[1536]{0:T(1024)S(1)}) fusion(f32[512]{0:T(512)S(1)} %bitcast.39, f32[512]{0:T(512)S(1)} %bitcast.42, f32[1536]{0:T(1024)S(1)} %get-tuple-element.215, f32[512]{0:T(512)S(1)} %bitcast.41, f32[1536]{0:T(1024)S(1)} %get-tuple-element.217, f32[512]{0:T(512)S(1)} %bitcast.43, ...), kind=kLoop, calls=%fused_computation.16.clone.1 | loop fusion | flops 24374784 | bytes 49152 | tf_op jit(solution)/shard_map/while/body/eval_jaxpr/reduce_sum | solution.py:24
  66.5 0.1 reshape.60
  66.6 0.1 copy.33
  66.7 0.7 reshape.64
  67.4 0.0 reduce-scatter.8.cloned.1.call-update
  67.4 0.0 reduce-scatter.10.cloned.1.call-start
  67.5 0.0 copy-done.1
  67.5 8.3 %all_gather.25 = f32[3,128,16]{2,1,0:T(8,128)S(1)} all-gather(f32[3,16,16]{2,1,0:T(8,128)S(1)} %copy-done.1), channel_id=1, replica_groups=mesh['tgt'=8,'src'=4] {'tgt'}, dimensions={1}, use_global_device_ids=true | all-gather | bytes 27648 | tf_op jit(solution)/shard_map/all_gather | solution.py:56
  75.8 11.1 %reduce-scatter.8.cloned.1.call-done = f32[16,48]{1,0:T(8,128)} async-done(((f32[64,48]{1,0:T(8,128)}), f32[16,48]{1,0:T(8,128)}) %reduce-scatter.8.cloned.1.call-update) | async-done | bytes 3088
  86.9 0.8 reshape.65
  87.7 0.1 copy.34
  87.8 9.1 %all_gather.26 = bf16[3,128,16]{2,1,0:T(8,128)(2,1)S(1)} all-gather(bf16[3,16,16]{2,1,0:T(8,128)(2,1)S(1)} %copy.34), channel_id=1, replica_groups=mesh['tgt'=8,'src'=4] {'tgt'}, dimensions={1}, use_global_device_ids=true | all-gather | bytes 13824 | tf_op jit(solution)/shard_map/all_gather | solution.py:75
  97.0 0.1 copy.30
  97.1 0.0 copy-start.3
  97.1 19.8 %fusion.16 = f32[1,3,16,64,1,1]{3,0,5,4,2,1:T(1,128)S(1)} fusion(bf16[3,128,16,1,1,1]{1,3,0,2,5,4:T(2,128)(2,1)S(1)} %copy.30, bf16[3,16,64,3,16,128]{5,4,3,2,1,0:T(8,128)(2,1)} %param.9), kind=kOutput, calls=%fused_computation.32 | convolution fusion | flops 37748736 | bytes 37773312 | tf_op jit(solution)/shard_map/xaqcbn,cnb->xaq/dot_general | solution.py:76
  116.8 0.1 copy.35
  117.0 0.7 reshape.66
  117.7 0.0 reduce-scatter.10.cloned.1.call-update
  117.8 0.1 sub.195
  117.8 0.1 sub.205
  117.9 0.1 sub.200
  118.0 0.1 reshape.59
  118.1 0.1 sub.202
  118.2 0.1 sub.207
  118.2 0.1 sub.197
  118.3 0.0 copy-done.3
  118.3 0.6 dynamic-slice
  119.6 14.7 %reduce-scatter.10.cloned.1.call-done = f32[16,48]{1,0:T(8,128)} async-done(((f32[64,48]{1,0:T(8,128)}), f32[16,48]{1,0:T(8,128)}) %reduce-scatter.10.cloned.1.call-update) | async-done | bytes 3088
  134.3 0.8 reshape.67
  135.1 0.1 copy.36
  135.2 0.0 copy-start.2
  135.2 9.4 %all_gather.27 = f32[3,128,16]{2,1,0:T(8,128)S(1)} all-gather(f32[3,16,16]{2,1,0:T(8,128)S(1)} %copy.36), channel_id=1, replica_groups=mesh['tgt'=8,'src'=4] {'tgt'}, dimensions={1}, use_global_device_ids=true | all-gather | bytes 27648 | tf_op jit(solution)/shard_map/all_gather | solution.py:80
  144.6 0.1 mul.306
  144.7 0.1 mul.309
  144.8 0.1 mul.302
  144.8 5.6 %fusion.24 = (f32[512]{0:T(512)S(1)}, f32[512]{0:T(512)S(1)}, f32[512]{0:T(512)S(1)}) fusion(f32[2048]{0:T(1024)S(1)} %mul.302, f32[2048]{0:T(1024)S(1)} %sub.197, f32[512]{0:T(512)S(1)} %sub.195, f32[2048]{0:T(1024)S(1)} %sub.207, f32[512]{0:T(512)S(1)} %sub.205, f32[2048]{0:T(1024)S(1)} %sub.202, f32[512]{0:T(512)S(1)} %sub.200, f32[2048]{0:T(1024)S(1)} %mul.309, ...), kind=kLoop, calls=%fused_computation.50 | loop fusion | flops 32504320 | bytes 61440 | tf_op jit(solution)/shard_map/while/body/eval_jaxpr/reduce_sum | solution.py:24
  150.4 0.1 stack.44
  150.5 0.1 stack.46
  150.6 0.1 stack.45
  150.7 15.9 %all-reduce = f32[3,8,64]{2,1,0:T(8,128)S(1)} all-reduce(f32[3,8,64]{2,1,0:T(8,128)S(1)} %fusion.34), channel_id=5, replica_groups=mesh['tgt'=8,'src'=4] {'src'}, use_global_device_ids=true, to_apply=%region_5.0.clone | all-reduce | flops 1536 | bytes 12288
  166.6 0.6 constant_dynamic-slice_fusion.2
  167.2 0.0 copy-done.2
  (20 shorter events, 0.2 us)
Async XLA Ops:
  7.2 24.8 %copy-start = (f32[64,64]{1,0:T(8,128)S(1)}, f32[64,64]{1,0:T(8,128)}, u32[]{:S(2)}) copy-start(f32[64,64]{1,0:T(8,128)} %param.8) | copy-start | bytes 49156
  7.2 79.8 %reduce-scatter.8.cloned.1.call-start = ((), (), s32[]{:S(2)}) async-start(), calls=%async_computation.2 | async-start | bytes 40960
  56.5 11.0 %copy-start.1 = (f32[3,16,16]{2,1,0:T(8,128)S(1)}, f32[3,16,16]{2,1,0:T(8,128)}, u32[]{:S(2)}) copy-start(f32[3,16,16]{2,1,0:T(8,128)} %param.7) | copy-start | bytes 9220
  67.4 66.9 %reduce-scatter.10.cloned.1.call-start = ((), (), s32[]{:S(2)}) async-start(), calls=%async_computation.3 | async-start | bytes 40960
  97.1 21.3 %copy-start.3 = (u32[32]{0:T(128)S(1)}, u32[32]{0:T(128)}, u32[]{:S(2)}) copy-start(u32[32]{0:T(128)} %constant.79) | copy-start | bytes 388
  135.2 32.0 %copy-start.2 = (f32[3,16,16]{2,1,0:T(8,128)}, f32[3,16,16]{2,1,0:T(8,128)S(1)}, u32[]{:S(2)}) copy-start(f32[3,16,16]{2,1,0:T(8,128)S(1)} %copy.36) | copy-start | bytes 9220
Sparse Core Ops, SparseCore 0:
  67.5 19.3 reduce-scatter.7
  117.8 16.4 reduce-scatter.9
where the time goes:
time: 174 us
  blocking collectives  89.2 us (51%)
  waiting for transfers between devices  25.9 us (15%)
  matrix products  20.6 us (12%)
  other arithmetic  15.1 us (9%)
  between operations  14.8 us (9%)
  local copies, waits for them, and re-layouts  8.12 us (5%)
    unnamed x4, waiting for transfers between devices  25.9 us
    dot_general x1, matrix products, per_device(): jnp.einsum('xaqcbn,cnb->xaq', shell_inverse, columns, preferred_element_t...  19.8 us
    unnamed x1, blocking collectives  15.9 us
    reduce_sum x3, other arithmetic, stokes_flow(): jnp.sum(diagonal_part * strength[0][None, :] + projection * delta_x, axis=1)  15 us
    all_gather x1, blocking collectives, per_device(): fibre_block = lax.all_gather(fibre_points, 'src', axis=1, tiled=True)  14.9 us
    all_gather x1, blocking collectives, per_device(): shell_rows = lax.all_gather(shell_points, 'src', axis=2, tiled=True)  13.3 us
    all_gather x1, blocking collectives, per_device(): column_density = lax.all_gather(density, 'tgt', axis=1, tiled=True)  9.42 us
    all_gather x1, blocking collectives, per_device(): lax.all_gather(shell_flow.astype(jnp.bfloat16), 'tgt', axis=1, tiled=True)  9.14 us
  transfers between devices with their start and end apart: 2, of which 2 were waited for; matrix products, arithmetic and copies ran while one was open for 1% of the time, Pallas kernels for 0%

commit v1 on v0

--- a/solution.py
+++ b/solution.py
@@ -6,6 +6,16 @@
 
 mobility = 1.0 / (8.0 * math.pi)
 soften_sq = 0.0025
+
+
+def pass_along(x, axis, d):
+    peers = lax.axis_size(axis)
+    held, blocks = (x, [x])
+    for _ in range(peers - 1):
+        held = lax.ppermute(held, axis, [(i, (i + 1) % peers) for i in range(peers)])
+        blocks.insert(0, held)
+    merged = jnp.concatenate(blocks, axis=d)
+    return jnp.roll(merged, (lax.axis_index(axis) + 1) * x.shape[d], axis=d)
 
 
 def stokes_flow(targets, sources, strength):
@@ -55,7 +65,7 @@
     shell_rows = lax.all_gather(shell_points, "src", axis=2, tiled=True)
     columns_pos = lax.all_gather(shell_points, "tgt", axis=1, tiled=True)
     forces = -jnp.einsum("cfm,nm->cfn", fibre_points, bending, precision=lax.Precision.HIGHEST)
-    fibre_block = lax.all_gather(fibre_points, "src", axis=1, tiled=True)
+    fibre_block = pass_along(fibre_points, "src", 1)
     block_flat = fibre_block.reshape(3, -1)
     targets = jnp.concatenate([block_flat, shell_rows.reshape(3, -1)], axis=1)
     zeros_flow = jnp.zeros(targets.shape, jnp.float32)

time: 174 us -> 176 us (1.011)
  blocking collectives: 89.2 us -> 74.6 us
  waiting for transfers between devices: 25.9 us -> 36.7 us
  starting transfers between devices: 0.08 us -> 4.35 us
    all_gather x1 -> x0, blocking collectives: 14.9 us -> none  [per_device(): fibre_block = lax.all_gather(fibre_points, 'src', axis=1, tiled=True)]
    unnamed x4, waiting for transfers between devices: 25.9 us -> 32.6 us
    ppermute x0 -> x3, starting transfers between devices: none -> 4.28 us  [pass_along(): lax.ppermute(held, axis, [(i, (i + 1) % peers) for i in range(peers)])]
    ppermute x0 -> x3, waiting for transfers between devices: none -> 4.1 us  [pass_along(): lax.ppermute(held, axis, [(i, (i + 1) % peers) for i in range(peers)])]
    unnamed x20 -> x18, local copies, waits for them, and re-layouts: 6.08 us -> 6.09 us
  transfers between devices with their start and end apart: 2 -> 5, of which waited for: 2 -> 3; matrix products, arithmetic and copies ran while one was open for 1% -> 2% of each run, Pallas kernels for 0% -> 0%
where the time goes in v1:
time: 176 us
  blocking collectives  74.6 us (42%)
  waiting for transfers between devices  36.7 us (21%)
  matrix products  20.6 us (12%)
  other arithmetic  15.1 us (9%)
  between operations  14.8 us (8%)
  local copies, waits for them, and re-layouts  9.52 us (5%)
  starting transfers between devices  4.35 us (2%)
    unnamed x4, waiting for transfers between devices  32.6 us
    dot_general x1, matrix products, per_device(): jnp.einsum('xaqcbn,cnb->xaq', shell_inverse, columns, preferred_element_t...  19.8 us
    unnamed x1, blocking collectives  15.9 us
    reduce_sum x3, other arithmetic, stokes_flow(): jnp.sum(diagonal_part * strength[0][None, :] + projection * delta_x, axis=1)  15 us
    all_gather x1, blocking collectives, per_device(): shell_rows = lax.all_gather(shell_points, 'src', axis=2, tiled=True)  13.6 us
    all_gather x1, blocking collectives, per_device(): columns_pos = lax.all_gather(shell_points, 'tgt', axis=1, tiled=True)  9.47 us
    all_gather x1, blocking collectives, per_device(): column_density = lax.all_gather(density, 'tgt', axis=1, tiled=True)  9.41 us
    all_gather x1, blocking collectives, per_device(): lax.all_gather(shell_flow.astype(jnp.bfloat16), 'tgt', axis=1, tiled=True)  9.11 us
  transfers between devices with their start and end apart: 5, of which 3 were waited for; matrix products, arithmetic and copies ran while one was open for 2% of the time, Pallas kernels for 0%

profile of v1, /device:TPU:0, one launch (start us, length us, event | category | flops | bytes accessed | tf_op | source)
XLA Modules:
  0.0 175.8 jit_solution(12620558292414480773)
XLA Ops:
  7.2 0.0 copy-start
  7.2 0.0 reduce-scatter.8.cloned.1.call-start
  7.2 3.1 %collective-permute-start = (f32[3,2,64]{2,1,0:T(2,128)}, f32[3,2,64]{2,1,0:T(2,128)S(1)}, u32[]{:S(2)}, u32[]{:S(2)}) collective-permute-start(f32[3,2,64]{2,1,0:T(2,128)} %param.6), channel_id=1, source_target_pairs={{0,1},{1,2},{2,3},{3,0},{4,5},{5,6},{6,7},{7,4},{8,9},{9,10},{10,1... | collective-permute-start | bytes 4616 | tf_op jit(solution)/shard_map/ppermute | solution.py:15
  10.3 0.7 copy.21
  11.0 0.8 copy.19
  11.9 9.5 %all_gather.21 = f32[3,128,16]{2,1,0:T(8,128)S(1)} all-gather(f32[3,16,16]{2,1,0:T(8,128)} %param.7), channel_id=1, replica_groups=mesh['tgt'=8,'src'=4] {'tgt'}, dimensions={1}, use_global_device_ids=true | all-gather | bytes 27648 | tf_op jit(solution)/shard_map/all_gather | solution.py:66
  21.3 0.8 convolution_negate_fusion
  22.2 13.6 %all_gather.18 = f32[3,16,64]{1,0,2:T(4,128)S(1)} all-gather(f32[3,16,16]{1,0,2:T(4,128)S(1)} %copy.19), channel_id=1, replica_groups=mesh['tgt'=8,'src'=4] {'src'}, dimensions={2}, use_global_device_ids=true | all-gather | bytes 15360 | tf_op jit(solution)/shard_map/all_gather | solution.py:65
  35.8 8.9 %all_gather.19 = f32[3,16,64]{2,0,1:T(4,128)S(1)} all-gather(f32[3,2,64]{2,0,1:T(4,128)S(1)} %copy.21), channel_id=1, replica_groups=mesh['tgt'=8,'src'=4] {'tgt'}, dimensions={1}, use_global_device_ids=true | all-gather | bytes 13824 | tf_op jit(solution)/shard_map/all_gather | solution.py:76
  44.6 0.0 collective-permute-done
  44.6 0.2 collective-permute-start.1
  44.9 8.3 %all_gather.20 = f32[3,16,64]{2,0,1:T(4,128)S(1)} all-gather(f32[3,2,64]{2,0,1:T(4,128)S(1)} %convolution_negate_fusion), channel_id=1, replica_groups=mesh['tgt'=8,'src'=4] {'tgt'}, dimensions={1}, use_global_device_ids=true | all-gather | bytes 13824 | tf_op jit(solution)/shard_map/all_gather | solution.py:77
  53.2 0.0 collective-permute-done.1
  53.2 0.9 collective-permute-start.2
  54.1 0.1 reshape.57
  54.2 0.1 reshape.58
  54.3 0.1 copy.20
  54.4 0.1 reshape.56
  54.5 4.1 %collective-permute-done.2 = f32[3,2,64]{2,1,0:T(2,128)S(1)} collective-permute-done((f32[3,2,64]{2,1,0:T(2,128)S(1)}, f32[3,2,64]{2,1,0:T(2,128)S(1)}, u32[]{:S(2)}, u32[]{:S(2)}) %collective-permute-start.2) | collective-permute-done | bytes 1568 | tf_op jit(solution)/shard_map/ppermute | solution.py:15
  58.6 1.4 concatenate.10
  60.0 0.1 reshape.55
  60.1 0.0 copy-start.2
  60.1 10.0 %while.9 = (s32[]{:T(128)}, f32[3,1536]{1,0:T(4,128)S(1)}, f32[3,1536]{1,0:T(4,128)S(1)}, f32[3,1024]{1,0:T(4,128)S(1)}, f32[3,1024]{1,0:T(4,128)S(1)}, /*index=...) while((s32[]{:T(128)}, f32[3,1536]{1,0:T(4,128)S(1)}, ...), condition=%wide.region_4.5_spmd.clone, body=%wide.region_0.4_spmd.clone.sunk | while | flops 24397832 | bytes 202961 | solution.py:57
  60.1 0.1 fusion.44
  60.2 0.1 slice_reduce_fusion.4
  60.3 4.7 %fusion.45 = (f32[1536]{0:T(1024)S(1)}, f32[1536]{0:T(1024)S(1)}, f32[1536]{0:T(1024)S(1)}) fusion(f32[512]{0:T(512)S(1)} %bitcast.39, f32[512]{0:T(512)S(1)} %bitcast.42, f32[1536]{0:T(1024)S(1)} %get-tuple-element.215, f32[512]{0:T(512)S(1)} %bitcast.41, f32[1536]{0:T(1024)S(1)} %get-tuple-element.217, f32[512]{0:T(512)S(1)} %bitcast.43, ...), kind=kLoop, calls=%fused_computation.16.clone.1 | loop fusion | flops 24374784 | bytes 49152 | tf_op jit(solution)/shard_map/while/body/eval_jaxpr/reduce_sum | solution.py:34
  65.1 0.1 fusion.44
  65.2 0.1 slice_reduce_fusion.4
  65.3 4.7 %fusion.45 = (f32[1536]{0:T(1024)S(1)}, f32[1536]{0:T(1024)S(1)}, f32[1536]{0:T(1024)S(1)}) fusion(f32[512]{0:T(512)S(1)} %bitcast.39, f32[512]{0:T(512)S(1)} %bitcast.42, f32[1536]{0:T(1024)S(1)} %get-tuple-element.215, f32[512]{0:T(512)S(1)} %bitcast.41, f32[1536]{0:T(1024)S(1)} %get-tuple-element.217, f32[512]{0:T(512)S(1)} %bitcast.43, ...), kind=kLoop, calls=%fused_computation.16.clone.1 | loop fusion | flops 24374784 | bytes 49152 | tf_op jit(solution)/shard_map/while/body/eval_jaxpr/reduce_sum | solution.py:34
  70.1 0.1 reshape.60
  70.2 0.1 copy.28
  70.3 0.7 reshape.64
  71.0 0.0 reduce-scatter.8.cloned.1.call-update
  71.0 0.0 reduce-scatter.10.cloned.1.call-start
  71.1 0.1 sub.207
  71.2 0.1 sub.212
  71.3 0.1 sub.202
  71.4 0.6 dynamic-slice
  72.6 16.3 %reduce-scatter.8.cloned.1.call-done = f32[16,48]{1,0:T(8,128)} async-done(((f32[64,48]{1,0:T(8,128)}), f32[16,48]{1,0:T(8,128)}) %reduce-scatter.8.cloned.1.call-update) | async-done | bytes 3088
  88.9 0.8 reshape.65
  89.7 0.1 copy.29
  89.8 9.1 %all_gather.22 = bf16[3,128,16]{2,1,0:T(8,128)(2,1)S(1)} all-gather(bf16[3,16,16]{2,1,0:T(8,128)(2,1)S(1)} %copy.29), channel_id=1, replica_groups=mesh['tgt'=8,'src'=4] {'tgt'}, dimensions={1}, use_global_device_ids=true | all-gather | bytes 13824 | tf_op jit(solution)/shard_map/all_gather | solution.py:85
  98.9 0.1 copy.25
  99.0 19.8 %fusion.16 = f32[1,3,16,64,1,1]{3,0,5,4,2,1:T(1,128)S(1)} fusion(bf16[3,128,16,1,1,1]{1,3,0,2,5,4:T(2,128)(2,1)S(1)} %copy.25, bf16[3,16,64,3,16,128]{5,4,3,2,1,0:T(8,128)(2,1)} %param.9), kind=kOutput, calls=%fused_computation.32 | convolution fusion | flops 37748736 | bytes 37773312 | tf_op jit(solution)/shard_map/xaqcbn,cnb->xaq/dot_general | solution.py:86
  118.7 0.1 copy.30
  118.9 0.7 reshape.66
  119.6 0.0 reduce-scatter.10.cloned.1.call-update
  119.6 0.1 sub.205
  119.7 0.1 sub.210
  119.8 0.1 sub.200
  119.9 0.1 reshape.59
  119.9 16.3 %reduce-scatter.10.cloned.1.call-done = f32[16,48]{1,0:T(8,128)} async-done(((f32[64,48]{1,0:T(8,128)}), f32[16,48]{1,0:T(8,128)}) %reduce-scatter.10.cloned.1.call-update) | async-done | bytes 3088
  136.2 0.8 reshape.67
  137.0 0.1 copy.31
  137.1 9.4 %all_gather.23 = f32[3,128,16]{2,1,0:T(8,128)S(1)} all-gather(f32[3,16,16]{2,1,0:T(8,128)S(1)} %copy.31), channel_id=1, replica_groups=mesh['tgt'=8,'src'=4] {'tgt'}, dimensions={1}, use_global_device_ids=true | all-gather | bytes 27648 | tf_op jit(solution)/shard_map/all_gather | solution.py:90
  146.5 0.1 mul.310
  146.6 0.1 mul.313
  146.7 0.1 mul.306
  146.8 5.5 %fusion.24 = (f32[512]{0:T(512)S(1)}, f32[512]{0:T(512)S(1)}, f32[512]{0:T(512)S(1)}) fusion(f32[2048]{0:T(1024)S(1)} %mul.306, f32[2048]{0:T(1024)S(1)} %sub.202, f32[512]{0:T(512)S(1)} %sub.200, f32[2048]{0:T(1024)S(1)} %sub.212, f32[512]{0:T(512)S(1)} %sub.210, f32[2048]{0:T(1024)S(1)} %sub.207, f32[512]{0:T(512)S(1)} %sub.205, f32[2048]{0:T(1024)S(1)} %mul.313, ...), kind=kLoop, calls=%fused_computation.50 | loop fusion | flops 32504320 | bytes 61440 | tf_op jit(solution)/shard_map/while/body/eval_jaxpr/reduce_sum | solution.py:34
  152.3 0.1 stack.44
  152.4 0.1 stack.46
  152.5 0.1 stack.45
  152.5 15.9 %all-reduce = f32[3,8,64]{2,1,0:T(8,128)S(1)} all-reduce(f32[3,8,64]{2,1,0:T(8,128)S(1)} %fusion.34), channel_id=5, replica_groups=mesh['tgt'=8,'src'=4] {'src'}, use_global_device_ids=true, to_apply=%region_5.6.clone | all-reduce | flops 1536 | bytes 12288
  168.4 0.6 constant_dynamic-slice_fusion.6
  (24 shorter events, 0.2 us)
Async XLA Ops:
  7.2 14.2 %copy-start = (f32[64,64]{1,0:T(8,128)S(1)}, f32[64,64]{1,0:T(8,128)}, u32[]{:S(2)}) copy-start(f32[64,64]{1,0:T(8,128)} %param.8) | copy-start | bytes 49156
  7.2 81.7 %reduce-scatter.8.cloned.1.call-start = ((), (), s32[]{:S(2)}) async-start(), calls=%async_computation.2 | async-start | bytes 40960
  7.2 37.4 %collective-permute-start = (f32[3,2,64]{2,1,0:T(2,128)}, f32[3,2,64]{2,1,0:T(2,128)S(1)}, u32[]{:S(2)}, u32[]{:S(2)}) collective-permute-start(f32[3,2,64]{2,1,0:T(2,128)} %param.6), channel_id=1, source_target_pairs={{0,1},{1,2},{2,3},{3,0},{4,5},{5,6},{6,7},{7,4},{8,9},{9,10},{10,1... | collective-permute-start | bytes 4616 | tf_op jit(solution)/shard_map/ppermute | solution.py:15
  44.6 8.5 %collective-permute-start.1 = (f32[3,2,64]{2,1,0:T(2,128)S(1)}, f32[3,2,64]{2,1,0:T(2,128)S(1)}, u32[]{:S(2)}, u32[]{:S(2)}) collective-permute-start(f32[3,2,64]{2,1,0:T(2,128)S(1)} %collective-permute-done), channel_id=1, source_target_pairs={{0,1},{1,2},{2,3},{3,0},{4,5},{5,6},{6,7},{7,4},{8,9},{9,10},{10,1... | collective-permute-start | bytes 4616 | tf_op jit(solution)/shard_map/ppermute | solution.py:15
  53.2 5.4 %collective-permute-start.2 = (f32[3,2,64]{2,1,0:T(2,128)S(1)}, f32[3,2,64]{2,1,0:T(2,128)S(1)}, u32[]{:S(2)}, u32[]{:S(2)}) collective-permute-start(f32[3,2,64]{2,1,0:T(2,128)S(1)} %collective-permute-done.1), channel_id=1, source_target_pairs={{0,1},{1,2},{2,3},{3,0},{4,5},{5,6},{6,7},{7,4},{8,9},{9,10},{10,1... | collective-permute-start | bytes 4616 | tf_op jit(solution)/shard_map/ppermute | solution.py:15
  60.1 11.3 %copy-start.2 = (u32[32]{0:T(128)S(1)}, u32[32]{0:T(128)}, u32[]{:S(2)}) copy-start(u32[32]{0:T(128)} %constant.108) | copy-start | bytes 388
  71.0 65.2 %reduce-scatter.10.cloned.1.call-start = ((), (), s32[]{:S(2)}) async-start(), calls=%async_computation.3 | async-start | bytes 40960
  137.1 31.9 %copy-start.1 = (f32[3,16,16]{2,1,0:T(8,128)}, f32[3,16,16]{2,1,0:T(8,128)S(1)}, u32[]{:S(2)}) copy-start(f32[3,16,16]{2,1,0:T(8,128)S(1)} %copy.31) | copy-start | bytes 9220
Sparse Core Ops, SparseCore 0:
  71.2 17.6 reduce-scatter.7
  119.7 16.4 reduce-scatter.9
